TPU v7x, 32 devices: a whole 2x2x4 slice. The times are simulated.
32 devices in a mesh: ka: 4 (over z), row: 8 (over y, x, core).
Axes of the slice: x: 2, y: 2, z: 4, core: 2. Of those that a mesh axis runs over, the one named last changes fastest.
Arguments:
- hamiltonian: float32 [16384, 4096], P(('ka', 'row')), parts along dimension 0, as said below
Outputs:
- sign_next: float32 [16384, 4096], P(('ka', 'row')), parts along dimension 0
- occupation: float32 [4], P('ka'), parts along dimension 0
There are 4 independent parts, one for each index of `ka`. A program takes and returns all parts, laid end to end along the dimension named above; each array names one. Nothing has to cross between parts.
Inputs may be any that keep to these rules, and one draw needn't show every extreme that they name: hamiltonian is symmetric up to float32 rounding.
All inputs are finite; a program needn't handle non-finite values.
Results may differ from a plain program's by a relative error of at most 0.0038.
Values may be sent and summed in bfloat16 or wider, within the bound.
A program may use at most 128 MiB of HBM per device.

v0:
```python
from functools import partial

import jax
import jax.numpy as jnp
from jax import lax
from jax.sharding import PartitionSpec as P


def multiply_rows(left, gathered):
    return jnp.dot(left, gathered, preferred_element_type=jnp.float32)


def own_diagonal(matrix, position, block_rows, cycle_size):
    shaped = matrix.reshape(block_rows, cycle_size, block_rows)
    square_block = lax.dynamic_slice_in_dim(shaped, position, 1, 1)[:, 0, :]
    return jnp.sum(jnp.diagonal(square_block))


def shards(hamiltonian):
    cycle_size = lax.axis_size("row")
    position = lax.axis_index("row")
    block_rows, order = hamiltonian.shape
    rounded = hamiltonian.astype(jnp.bfloat16)
    gathered = lax.all_gather(rounded, "row", axis=0, tiled=True)
    multiply = partial(multiply_rows, gathered=gathered)
    square_low = multiply(rounded).astype(jnp.bfloat16)
    cube = multiply(square_low)
    sign_next = 1.5 * hamiltonian - 0.5 * cube
    total = lax.psum(own_diagonal(sign_next, position, block_rows, cycle_size), "row")
    occupation = jnp.reshape(0.5 - total / (2.0 * order), (1,))
    return (sign_next, occupation)


def solution(mesh):
    placed = (P(("ka", "row"), None),)
    return jax.shard_map(
        shards,
        mesh=mesh,
        in_specs=placed,
        out_specs=(P(("ka", "row"), None), P("ka")),
        check_vma=False,
    )
```

profile of v0, /device:TPU:0, one launch (start us, length us, event | category | flops | bytes accessed | tf_op | source)
XLA Modules:
  0.0 269.6 jit_solution(1665986670191946976)
XLA Ops:
  7.2 0.0 all-gather.2.cloned.1.call-start
  7.2 6.0 %convert_element_type.6 = bf16[512,4096]{1,0:T(8,128)(2,1)} convert(f32[512,4096]{1,0:T(8,128)} %param.1) | non-fusion elementwise | flops 2097152 | bytes 12582912 | tf_op jit(solution)/shard_map/convert_element_type | solution.py:23
  13.2 0.0 all-gather.2.cloned.1.call-update
  13.3 163.5 %all-gather.2.cloned.1.call-done = bf16[4096,4096]{1,0:T(8,128)(2,1)} async-done(((bf16[512,4096]{1,0:T(8,128)(2,1)}), bf16[4096,4096]{1,0:T(8,128)(2,1)}) %all-gather.2.cloned.1.call-update) | async-done | bytes 33554448 | tf_op jit(solution)/shard_map/all_gather | solution.py:24
  176.8 24.8 %convolution_convert_fusion.clone.4 = bf16[512,4096]{1,0:T(8,128)(2,1)} fusion(bf16[4096,4096]{1,0:T(8,128)(2,1)} %all-gather.2.cloned.1.call-done, f32[512,4096]{1,0:T(8,128)} %param.1), kind=kOutput, calls=%fused_computation.2.clone.clone.clone.1 | convolution fusion | flops 17184063488 | bytes 46137344 | tf_op jit(solution)/shard_map/dot_general | solution.py:10
  201.6 27.9 %multiply_subtract_fusion = f32[512,4096]{1,0:T(8,128)} fusion(f32[512,4096]{1,0:T(8,128)} %param.1, bf16[4096,4096]{1,0:T(8,128)(2,1)} %all-gather.2.cloned.1.call-done, bf16[512,4096]{1,0:T(8,128)(2,1)} %convolution_convert_fusion.clone.4), kind=kOutput, calls=%fused_computation.1 | convolution fusion | flops 17186160640 | bytes 54525952 | tf_op jit(solution)/shard_map/dot_general | solution.py:10
  229.5 11.5 %copy.4 = f32[64,8,8,512]{3,2,1,0:T(8,128)S(1)} copy(f32[64,8,8,512]{3,1,2,0:T(8,128)} %bitcast.17) | data formatting | bytes 16777216
  241.0 1.1 constant_dynamic-slice_fusion
  242.1 0.1 copy.6
  242.1 4.5 %gather_fusion = f32[512]{0:T(512)S(1)} fusion(f32[512,512]{1,0:T(8,128)S(1)} %bitcast.16, s32[512]{0:T(512)S(1)} %bitcast.14), kind=kCustom, calls=%fused_computation | custom fusion | bytes 8192 | tf_op jit(solution)/shard_map/jit(diagonal)/cond/branch_0_fun/gather | solution.py:16
  246.7 0.6 reduce_sum.9
  247.3 13.7 %psum.7 = f32[]{:T(128)} all-reduce(f32[]{:T(128)} %reduce_sum.9), channel_id=1, replica_groups=mesh['ka'=4,'row'=8] {'row'}, use_global_device_ids=true, to_apply=%region_1.2 | all-reduce | flops 1 | bytes 8 | tf_op jit(solution)/shard_map/psum | solution.py:29
  (1 shorter events, 0.0 us)
Async XLA Ops:
  7.2 169.6 %all-gather.2.cloned.1.call-start = ((), (), s32[]{:S(2)}) async-start(), calls=%async_computation | async-start | bytes 37748736 | tf_op jit(solution)/shard_map/all_gather | solution.py:24
Sparse Core Ops, SparseCore 0:
  13.4 163.3 all-gather.1
where the time goes:
time: 270 us
  waiting for transfers between devices  164 us (61%)
  matrix products  52.7 us (20%)
  local copies, waits for them, and re-layouts  17.1 us (6%)
  between operations  15.8 us (6%)
  blocking collectives  13.7 us (5%)
  other arithmetic  6.63 us (2%)
    all_gather x1, waiting for transfers between devices, shards(): gathered = lax.all_gather(rounded, 'row', axis=0, tiled=True)  164 us
    dot_general x2, matrix products, multiply_rows(): return jnp.dot(left, gathered, preferred_element_type=jnp.float32)  52.7 us
    psum x1, blocking collectives, shards(): lax.psum(own_diagonal(sign_next, position, block_rows, cycle_size), 'row')  13.7 us
    unnamed x2, local copies, waits for them, and re-layouts  11.6 us
    convert_element_type x1, other arithmetic, shards(): rounded = hamiltonian.astype(jnp.bfloat16)  6.03 us
  transfers between devices with their start and end apart: 1, of which 1 were waited for; matrix products, arithmetic and copies ran while one was open for 0% of the time, Pallas kernels for 0%

commit v1 on v0

--- a/solution.py
+++ b/solution.py
@@ -3,7 +3,13 @@
 import jax
 import jax.numpy as jnp
 from jax import lax
+from jax.experimental import pallas as pl
+from jax.experimental.pallas import tpu as pltpu
 from jax.sharding import PartitionSpec as P
+
+MESH = pl.DeviceIdType.MESH
+PLANE = (2, 2, 2)
+MESSAGES = 6
 
 
 def multiply_rows(left, gathered):
@@ -16,7 +22,7 @@
     return jnp.sum(jnp.diagonal(square_block))
 
 
-def shards(hamiltonian):
+def gathered_shards(hamiltonian):
     cycle_size = lax.axis_size("row")
     position = lax.axis_index("row")
     block_rows, order = hamiltonian.shape
@@ -31,7 +37,344 @@
     return (sign_next, occupation)
 
 
+def kernel(
+    rounded_hbm, ham_hbm, out_hbm, occ_ref,
+    g, s_low, s_acc, c_acc, tr,
+    load_sem, out_sem, p_send, p_recv, x_send, x_recv, y_send, y_recv,
+    f_send, f_recv, dx_send, dx_recv, dy_send, dy_recv, df_send, df_recv,
+    t_send, t_recv,
+):
+    nb, order = rounded_hbm.shape
+    half, wide, tile = nb // 2, 2 * nb, nb // 2
+    pos = lax.axis_index("row")
+    n_dev = lax.axis_size("row")
+    chip, core = pos // 2, pos % 2
+    y, x = chip // 2, chip % 2
+
+    def chip_at(ry, rx, base=None):
+        by, bx = (y, x) if base is None else base
+        return (by + ry - 2 * by * ry, bx + rx - 2 * bx * rx)
+
+    def index(at):
+        return at[0] * 2 + at[1]
+
+    here = (y, x)
+    near_x, near_y, far = chip_at(0, 1), chip_at(1, 0), chip_at(1, 1)
+    partner = pos + 1 - 2 * core
+
+    def al(v, m=tile):
+        return pl.multiple_of(v, m)
+
+    def loc(axis, m, at, a):
+        c = index(at)
+        mine = (2 * c + a) * nb
+        if m == 0:
+            other = index(chip_at(1, 1, at))
+            col = (2 * other + (a if axis == "x" else 1 - a)) * nb
+            return pl.ds(al(mine), nb), pl.ds(al(col), nb)
+        if m == 1:
+            return pl.ds(al(mine), half), pl.ds(al(mine), nb)
+        if m == 2:
+            return pl.ds(al(mine + half), half), pl.ds(al(mine + half), half)
+        if m == 3:
+            return (
+                pl.ds(al(2 * c * nb + a * half), half),
+                pl.ds(al((2 * c + 1) * nb), nb),
+            )
+        other = index(chip_at(1, 0, at) if axis == "x" else chip_at(0, 1, at))
+        return pl.ds(al(mine), nb), pl.ds(al((2 * other + m - 4) * nb), nb)
+
+    def copy(where, target, send, recv):
+        ref = g.at[where[0], where[1]]
+        return pltpu.make_async_remote_copy(
+            src_ref=ref, dst_ref=ref, send_sem=send, recv_sem=recv,
+            device_id={"row": target}, device_id_type=MESH,
+        )
+
+    to_x = 2 * index(near_x) + core
+    to_y = 2 * index(near_y) + core
+    pass_from = (
+        near_x[0] + core * (near_y[0] - near_x[0]),
+        near_x[1] + core * (near_y[1] - near_x[1]),
+    )
+    to_pass = to_y + core * (to_x - to_y)
+
+    def own(axis, m):
+        sems = (x_send, x_recv) if axis == "x" else (y_send, y_recv)
+        return copy(loc(axis, m, here, core), to_x if axis == "x" else to_y,
+                    sems[0].at[m], sems[1].at[m])
+
+    def arriving(axis, m):
+        sems = (x_send, x_recv) if axis == "x" else (y_send, y_recv)
+        return copy(loc(axis, m, near_x if axis == "x" else near_y, core),
+                    to_x if axis == "x" else to_y, sems[0].at[m], sems[1].at[m])
+
+    def shared(axis, m, a):
+        sems = (dx_send, dx_recv) if axis == "x" else (dy_send, dy_recv)
+        return copy(loc(axis, m, near_x if axis == "x" else near_y, a),
+                    partner, sems[0].at[m], sems[1].at[m])
+
+    def passed(m, at):
+        return copy(loc("x", m, at, core), to_pass, f_send.at[m - 1], f_recv.at[m - 1])
+
+    def passed_shared(m, a):
+        return copy(loc("x", m, far, a), partner, df_send.at[m - 1], df_recv.at[m - 1])
+
+    my_rows = pl.ds(al(pos * nb), nb)
+    load = pltpu.make_async_copy(rounded_hbm, g.at[my_rows, :], load_sem.at[0])
+    load.start()
+    load_h = pltpu.make_async_copy(ham_hbm, c_acc, load_sem.at[1])
+    load_h.start()
+    barrier = pltpu.get_barrier_semaphore()
+    for k in range(1, 8):
+        pl.semaphore_signal(barrier, inc=1, device_id={"row": (pos + k) % n_dev},
+                            device_id_type=MESH)
+    pl.semaphore_wait(barrier, 7)
+    load.wait()
+    whole = copy((my_rows, slice(None)), partner, p_send, p_recv)
+    for m in range(3):
+        own("x", m).start()
+        own("y", m).start()
+    whole.start()
+
+    f32 = jnp.float32
+
+    def nn(left, right):
+        return lax.dot_general(left, right, (((1,), (0,)), ((), ())),
+                               preferred_element_type=f32)
+
+    def nt(left, right):
+        return lax.dot_general(left, right, (((1,), (1,)), ((), ())),
+                               preferred_element_type=f32)
+
+    left = g.at[my_rows, :]
+    mine = pl.ds(al(pos * nb), nb)
+    home = pl.ds(al(chip * wide), wide)
+    load_h.wait()
+
+    def eye():
+        return (lax.broadcasted_iota(jnp.int32, (nb, nb), 0)
+                == lax.broadcasted_iota(jnp.int32, (nb, nb), 1))
+
+    tr_h = jnp.sum(jnp.where(eye(), c_acc[:, mine], 0.0), axis=0, keepdims=True)
+    s_acc[0:1, mine] = tr_h
+
+    whole_in = copy((pl.ds(al(partner * nb), nb), slice(None)), partner, p_send, p_recv)
+    whole_in.wait_recv()
+    for m in range(3, MESSAGES):
+        own("x", m).start()
+        own("y", m).start()
+    tr[pos, 0:1, :] = s_acc[0:1, mine]
+
+    @pl.loop(0, wide // tile)
+    def _(t):
+        at = al(chip * wide + t * tile)
+        s_low[:, pl.ds(at, tile)] = nt(left[...], g[pl.ds(at, tile), :]).astype(jnp.bfloat16)
+
+    def chip_rel(r):
+        return chip_at(r // 2, r % 2)
+
+    def forward_ready(axis, m):
+        arriving(axis, m).wait_recv()
+        shared(axis, m, core).start()
+
+    per_chip = wide // tile
+
+    @pl.loop(0, 3 * per_chip)
+    def _(t):
+        at = al(index(chip_rel(1 + t // per_chip)) * wide + (t % per_chip) * tile)
+        s_acc[:, pl.ds(at, tile)] = nn(left[:, home], g[home, pl.ds(at, tile)])
+
+    @pl.loop(0, order // tile)
+    def _(t):
+        cols = pl.ds(al(t * tile), tile)
+        c_acc[:, cols] = -3.0 * c_acc[:, cols] + nn(s_low[:, home], g[home, cols])
+
+    for m in range(3):
+        forward_ready("x", m)
+        forward_ready("y", m)
+    for m in (1, 2):
+        passed(m, pass_from).start()
+
+    def add_pair(dst, lhs, i, j):
+        rows, cols = pl.ds(al(i * nb), nb), pl.ds(al(j * nb), nb)
+        dst[:, cols] += nn(lhs[:, rows], g[rows, cols])
+        dst[:, rows] += nt(lhs[:, cols], g[rows, cols])
+
+    nx, ny, nf = 2 * index(near_x), 2 * index(near_y), 2 * index(far)
+
+    def add_cross(dst, lhs):
+        @pl.loop(0, 4)
+        def _(t):
+            a, kind = t % 2, t // 2
+            i = nx + a + kind * (ny - nx)
+            j = ny + a + kind * (nx + 1 - a - ny - a)
+            add_pair(dst, lhs, i, j)
+
+    def add_diagonal(dst, lhs, base):
+        rows = pl.ds(al(base * nb), wide)
+        for t in range(per_chip):
+            cols = pl.ds(al(base * nb + t * tile), tile)
+            dst[:, cols] += nn(lhs[:, rows], g[rows, cols])
+
+    def mirror_diagonal(base):
+        low = al(base * nb)
+        for b in range(2):
+            at = low + b * nb
+            g[pl.ds(al(at + half), half), pl.ds(al(at), half)] = (
+                g[pl.ds(al(at), half), pl.ds(al(at + half), half)].T)
+        for b in range(2):
+            g[pl.ds(al(low + nb), nb), pl.ds(al(low + b * half), half)] = (
+                g[pl.ds(al(low + b * half), half), pl.ds(al(low + nb), nb)].T)
+
+    def wait_shared(m):
+        shared("x", m, 1 - core).wait_recv()
+        shared("y", m, 1 - core).wait_recv()
+
+    wait_shared(0)
+    add_cross(s_acc, left)
+    forward_ready("x", 3)
+    forward_ready("y", 3)
+    passed(3, pass_from).start()
+    for m in (1, 2, 3):
+        wait_shared(m)
+
+    @pl.loop(0, 2)
+    def _(t):
+        base = nx + t * (ny - nx)
+        mirror_diagonal(base)
+        add_diagonal(s_acc, left, base)
+
+    for m in (4, 5):
+        forward_ready("x", m)
+        forward_ready("y", m)
+        wait_shared(m)
+
+        @pl.loop(0, 4)
+        def _(t):
+            i = nx + t % 2 + (t // 2) * (ny - nx)
+            add_pair(s_acc, left, i, nf + m - 4)
+
+    @pl.loop(0, 2)
+    def _(t):
+        base = nx + t * (ny - nx)
+        part = pl.ds(al(base * nb), wide)
+        s_low[:, part] = s_acc[:, part].astype(jnp.bfloat16)
+
+    add_cross(c_acc, s_low)
+
+    @pl.loop(0, 2)
+    def _(t):
+        base = nx + t * (ny - nx)
+        part = pl.ds(al(base * nb), wide)
+        add_diagonal(c_acc, s_low, base)
+        for b in range(2):
+            rows = pl.ds(al((2 * chip + b) * nb), nb)
+            c_acc[:, rows] += nt(s_low[:, part], g[rows, part])
+        for k in range(per_chip):
+            cols = pl.ds(al(nf * nb + k * tile), tile)
+            c_acc[:, cols] += nn(s_low[:, part], g[part, cols])
+
+    for m in (1, 2, 3):
+        passed(m, far).wait_recv()
+        passed_shared(m, core).start()
+    for m in (1, 2, 3):
+        passed_shared(m, 1 - core).wait_recv()
+    last = pl.ds(al(nf * nb), wide)
+    mirror_diagonal(nf)
+    add_diagonal(s_acc, left, nf)
+    s_low[:, last] = s_acc[:, last].astype(jnp.bfloat16)
+
+    def trace_step(t, carry):
+        cols = pl.ds(al(t * nb), nb)
+        product = s_low[:, cols].astype(f32) * left[:, cols].astype(f32)
+        return carry + jnp.sum(product, axis=0, keepdims=True)
+
+    tr_c = lax.fori_loop(0, order // nb, trace_step, jnp.zeros((1, nb), f32))
+    tr[pos, 0:1, :] = 1.5 * tr[pos, 0:1, :] - 0.5 * tr_c
+
+    def finish(i):
+        cols = pl.ds(al(i * nb), nb)
+        return pltpu.make_async_copy(c_acc.at[:, cols], out_hbm.at[:, cols], out_sem.at[i])
+
+    for b in range(2):
+        cols = pl.ds(al((nf + b) * nb), nb)
+        c_acc[:, cols] = -0.5 * (c_acc[:, cols] + nn(s_low[:, last], g[last, cols]))
+        finish(nf + b).start()
+
+    def trace_copy(k, slot):
+        return pltpu.make_async_remote_copy(
+            src_ref=tr.at[slot], dst_ref=tr.at[slot],
+            send_sem=t_send.at[k - 1], recv_sem=t_recv.at[k - 1],
+            device_id={"row": (pos + k) % n_dev}, device_id_type=MESH,
+        )
+
+    for k in range(1, 8):
+        trace_copy(k, pos).start()
+
+    @pl.loop(0, 6)
+    def _(t):
+        i = 2 * index(chip_rel(t // 2)) + t % 2
+        rows = pl.ds(al(i * nb), nb)
+        c_acc[:, rows] = -0.5 * (c_acc[:, rows] + nt(s_low[:, last], g[rows, last]))
+        finish(i).start()
+
+    for k in range(1, 8):
+        trace_copy(k, (pos + n_dev - k) % n_dev).wait_recv()
+    total = jnp.sum(tr[:, 0:1, :])
+    occ_ref[...] = jnp.full(occ_ref.shape, 0.5 - total / (2.0 * order), f32)
+
+    for k in range(1, 8):
+        trace_copy(k, pos).wait_send()
+    whole.wait_send()
+    for m in range(MESSAGES):
+        for axis in ("x", "y"):
+            own(axis, m).wait_send()
+            shared(axis, m, core).wait_send()
+    for m in (1, 2, 3):
+        passed(m, pass_from).wait_send()
+        passed_shared(m, core).wait_send()
+
+    @pl.loop(0, order // nb)
+    def _(i):
+        finish(i).wait()
+
+
+def symmetric_shards(hamiltonian):
+    nb, order = hamiltonian.shape
+    cycle_size = lax.axis_size("row")
+    dma = pltpu.SemaphoreType.DMA
+    six, three, seven = dma((MESSAGES,)), dma((3,)), dma((cycle_size - 1,))
+    hbm = pl.BlockSpec(memory_space=pl.ANY)
+    sign_next, occupation = pl.pallas_call(
+        kernel,
+        out_shape=(
+            jax.ShapeDtypeStruct((nb, order), jnp.float32),
+            jax.ShapeDtypeStruct((8, 128), jnp.float32),
+        ),
+        in_specs=[hbm, hbm],
+        out_specs=(hbm, pl.BlockSpec(memory_space=pltpu.VMEM)),
+        scratch_shapes=[
+            pltpu.VMEM((order, order), jnp.bfloat16),
+            pltpu.VMEM((nb, order), jnp.bfloat16),
+            pltpu.VMEM((nb, order), jnp.float32),
+            pltpu.VMEM((nb, order), jnp.float32),
+            pltpu.VMEM((cycle_size, 8, nb), jnp.float32),
+            dma((2,)), dma((cycle_size,)), dma, dma,
+            six, six, six, six, three, three,
+            six, six, six, six, three, three,
+            seven, seven,
+        ],
+        compiler_params=pltpu.CompilerParams(
+            collective_id=0, has_side_effects=True, vmem_limit_bytes=67043328,
+        ),
+    )(hamiltonian.astype(jnp.bfloat16), hamiltonian)
+    return (sign_next, occupation[0, :1])
+
+
 def solution(mesh):
+    plane = PLANE[0] * PLANE[1] * PLANE[2]
+    shards = symmetric_shards if mesh.shape["row"] == plane else gathered_shards
     placed = (P(("ka", "row"), None),)
     return jax.shard_map(
         shards,

time: 270 us -> 98.9 us (0.37)
  waiting for transfers between devices: 164 us -> 0 us
  Pallas kernels: 0 us -> 83 us
  matrix products: 52.7 us -> 0 us
  between operations: 15.8 us -> 0.64 us
  blocking collectives: 13.7 us -> 0 us
  local copies, waits for them, and re-layouts: 17.1 us -> 8.97 us
    all_gather x1 -> x0, waiting for transfers between devices: 164 us -> none  [shards(): gathered = lax.all_gather(rounded, 'row', axis=0, tiled=True)]
    pallas_call x0 -> x1, Pallas kernels: none -> 83 us  [symmetric_shards(): pl.pallas_call(kernel, out_shape=(jax.ShapeDtypeStruct((nb, order), jnp.f...]
    dot_general x2 -> x0, matrix products: 52.7 us -> none  [multiply_rows(): return jnp.dot(left, gathered, preferred_element_type=jnp.float32)]
    psum x1 -> x0, blocking collectives: 13.7 us -> none  [shards(): lax.psum(own_diagonal(sign_next, position, block_rows, cycle_size), 'row')]
    gather x1 -> x0, local copies, waits for them, and re-layouts: 4.52 us -> none  [own_diagonal(): return jnp.sum(jnp.diagonal(square_block))]
    unnamed x2 -> x1, local copies, waits for them, and re-layouts: 11.6 us -> 7.77 us
  transfers between devices with their start and end apart: 1 -> 0, of which waited for: 1 -> 0; matrix products, arithmetic and copies ran while one was open for 0% -> 0% of each run, Pallas kernels for 0% -> 0%
where the time goes in v1:
time: 98.9 us; the launch traced here: 98.6 us
  Pallas kernels  83 us (84%)
  local copies, waits for them, and re-layouts  8.97 us (9%)
  other arithmetic  6.03 us (6%)
    pallas_call x1, Pallas kernels, symmetric_shards(): pl.pallas_call(kernel, out_shape=(jax.ShapeDtypeStruct((nb, order), jnp.f...  83 us
    unnamed x1, local copies, waits for them, and re-layouts  7.77 us
    convert_element_type x1, other arithmetic, symmetric_shards(): hamiltonian.astype(jnp.bfloat16)  6.03 us

profile of v1, /device:TPU:0, one launch (start us, length us, event | category | flops | bytes accessed | tf_op | source)
XLA Modules:
  0.0 98.6 jit_solution(3677515936115431718)
XLA Ops:
  0.6 6.0 %convert_element_type.3.rounded_hbm = bf16[512,4096]{1,0:T(8,128)(2,1)} convert(f32[512,4096]{1,0:T(8,128)} %ham_hbm.1) | non-fusion elementwise | flops 2097152 | bytes 12582912 | tf_op jit(solution)/shard_map/convert_element_type | solution.py:371
  6.7 83.0 %shard_map.30 = (f32[512,4096]{1,0:T(8,128)}, f32[8,128]{1,0:T(8,128)}) custom-call(bf16[512,4096]{1,0:T(8,128)(2,1)} %convert_element_type.3.rounded_hbm, f32[512,4096]{1,0:T(8,128)} %ham_hbm.1), custom_call_target="tpu_custom_call" | custom-call | tf_op jit(solution)/shard_map/pallas_call | solution.py:349
  89.7 1.2 %slice.3 = f32[1,1]{1,0:T(1,128)} slice(f32[8,128]{1,0:T(8,128)} %get-tuple-element.5), slice={[0:1], [0:1]} | slice | bytes 8 | tf_op jit(solution)/shard_map/slice | solution.py:372
  90.9 7.8 %copy.4 = f32[512,4096]{1,0:T(8,128)} copy(f32[512,4096]{1,0:T(8,128)} %get-tuple-element.8) | data formatting | bytes 16777216

commit v2 on v1

--- a/solution.py
+++ b/solution.py
@@ -38,13 +38,13 @@
 
 
 def kernel(
-    rounded_hbm, ham_hbm, out_hbm, occ_ref,
-    g, s_low, s_acc, c_acc, tr,
-    load_sem, out_sem, p_send, p_recv, x_send, x_recv, y_send, y_recv,
+    ham_hbm, c_acc, occ_ref,
+    g, s_low, s_acc, tr,
+    load_sem, p_send, p_recv, x_send, x_recv, y_send, y_recv,
     f_send, f_recv, dx_send, dx_recv, dy_send, dy_recv, df_send, df_recv,
     t_send, t_recv,
 ):
-    nb, order = rounded_hbm.shape
+    nb, order = ham_hbm.shape
     half, wide, tile = nb // 2, 2 * nb, nb // 2
     pos = lax.axis_index("row")
     n_dev = lax.axis_size("row")
@@ -82,7 +82,8 @@
                 pl.ds(al((2 * c + 1) * nb), nb),
             )
         other = index(chip_at(1, 0, at) if axis == "x" else chip_at(0, 1, at))
-        return pl.ds(al(mine), nb), pl.ds(al((2 * other + m - 4) * nb), nb)
+        row = (2 * c + m - 4) * nb + a * half
+        return pl.ds(al(row), half), pl.ds(al(other * wide), wide)
 
     def copy(where, target, send, recv):
         ref = g.at[where[0], where[1]]
@@ -121,20 +122,38 @@
         return copy(loc("x", m, far, a), partner, df_send.at[m - 1], df_recv.at[m - 1])
 
     my_rows = pl.ds(al(pos * nb), nb)
-    load = pltpu.make_async_copy(rounded_hbm, g.at[my_rows, :], load_sem.at[0])
-    load.start()
-    load_h = pltpu.make_async_copy(ham_hbm, c_acc, load_sem.at[1])
-    load_h.start()
+    pieces = []
+    for k, at in enumerate((far, here, near_x, near_y)):
+        cols = pl.ds(al(index(at) * wide), wide)
+        load = pltpu.make_async_copy(ham_hbm.at[:, cols], c_acc.at[:, cols], load_sem.at[k])
+        load.start()
+        pieces.append((cols, load))
+
+    def round_piece(k):
+        cols, load = pieces[k]
+        load.wait()
+
+        @pl.loop(0, nb // 32)
+        def _(t):
+            rows = pl.ds(pl.multiple_of(t * 32, 32), 32)
+            to = pl.ds(pl.multiple_of(pos * nb + t * 32, 32), 32)
+            g[to, cols] = c_acc[rows, cols].astype(jnp.bfloat16)
+
     barrier = pltpu.get_barrier_semaphore()
     for k in range(1, 8):
         pl.semaphore_signal(barrier, inc=1, device_id={"row": (pos + k) % n_dev},
                             device_id_type=MESH)
+    round_piece(0)
+    round_piece(1)
     pl.semaphore_wait(barrier, 7)
-    load.wait()
-    whole = copy((my_rows, slice(None)), partner, p_send, p_recv)
-    for m in range(3):
+    own("x", 0).start()
+    own("y", 0).start()
+    round_piece(2)
+    round_piece(3)
+    for m in (1, 2):
         own("x", m).start()
         own("y", m).start()
+    whole = copy((my_rows, slice(None)), partner, p_send, p_recv)
     whole.start()
 
     f32 = jnp.float32
@@ -150,7 +169,6 @@
     left = g.at[my_rows, :]
     mine = pl.ds(al(pos * nb), nb)
     home = pl.ds(al(chip * wide), wide)
-    load_h.wait()
 
     def eye():
         return (lax.broadcasted_iota(jnp.int32, (nb, nb), 0)
@@ -245,39 +263,48 @@
         mirror_diagonal(base)
         add_diagonal(s_acc, left, base)
 
-    for m in (4, 5):
-        forward_ready("x", m)
-        forward_ready("y", m)
-        wait_shared(m)
+    def block(k):
+        return pl.ds(al(k * nb), nb)
+
+    def add_column(q, base):
+        for k in range(2):
+            to = block(2 * chip + k)
+            c_acc[:, to] += nt(s_low[:, block(q)], g[to, block(q)])
+        for start in (nf, base):
+            for k in range(2):
+                to = block(start + k)
+                c_acc[:, to] += nn(s_low[:, block(q)], g[block(q), to])
+
+    for b in range(2):
+        forward_ready("x", 4 + b)
+        forward_ready("y", 4 + b)
+        wait_shared(4 + b)
 
         @pl.loop(0, 4)
         def _(t):
-            i = nx + t % 2 + (t // 2) * (ny - nx)
-            add_pair(s_acc, left, i, nf + m - 4)
-
-    @pl.loop(0, 2)
-    def _(t):
-        base = nx + t * (ny - nx)
-        part = pl.ds(al(base * nb), wide)
-        s_low[:, part] = s_acc[:, part].astype(jnp.bfloat16)
-
-    add_cross(c_acc, s_low)
-
-    @pl.loop(0, 2)
-    def _(t):
-        base = nx + t * (ny - nx)
-        part = pl.ds(al(base * nb), wide)
-        add_diagonal(c_acc, s_low, base)
-        for b in range(2):
-            rows = pl.ds(al((2 * chip + b) * nb), nb)
-            c_acc[:, rows] += nt(s_low[:, part], g[rows, part])
-        for k in range(per_chip):
-            cols = pl.ds(al(nf * nb + k * tile), tile)
-            c_acc[:, cols] += nn(s_low[:, part], g[part, cols])
-
-    for m in (1, 2, 3):
-        passed(m, far).wait_recv()
-        passed_shared(m, core).start()
+            add_pair(s_acc, left, nx + b + (t // 2) * (ny - nx), nf + t % 2)
+
+        qx, qy = nx + b, ny + b
+        for q in (qx, qy):
+            s_low[:, block(q)] = s_acc[:, block(q)].astype(jnp.bfloat16)
+        c_acc[:, block(qy)] += nn(s_low[:, block(qx)], g[block(qx), block(qy)])
+        c_acc[:, block(qx)] += nt(s_low[:, block(qy)], g[block(qx), block(qy)])
+        c_acc[:, block(ny + 1 - b)] += nt(
+            s_low[:, block(qx)], g[block(ny + 1 - b), block(qx)])
+        c_acc[:, block(nx + 1 - b)] += nn(
+            s_low[:, block(qy)], g[block(qy), block(nx + 1 - b)])
+        if b == 0:
+            @pl.loop(0, 2)
+            def _(t):
+                base = nx + t * (ny - nx)
+                add_column(base + b, base)
+        else:
+            add_column(nx + b, nx)
+            for m in (1, 2, 3):
+                passed(m, far).wait_recv()
+                passed_shared(m, core).start()
+            add_column(ny + b, ny)
+
     for m in (1, 2, 3):
         passed_shared(m, 1 - core).wait_recv()
     last = pl.ds(al(nf * nb), wide)
@@ -293,14 +320,9 @@
     tr_c = lax.fori_loop(0, order // nb, trace_step, jnp.zeros((1, nb), f32))
     tr[pos, 0:1, :] = 1.5 * tr[pos, 0:1, :] - 0.5 * tr_c
 
-    def finish(i):
-        cols = pl.ds(al(i * nb), nb)
-        return pltpu.make_async_copy(c_acc.at[:, cols], out_hbm.at[:, cols], out_sem.at[i])
-
     for b in range(2):
         cols = pl.ds(al((nf + b) * nb), nb)
         c_acc[:, cols] = -0.5 * (c_acc[:, cols] + nn(s_low[:, last], g[last, cols]))
-        finish(nf + b).start()
 
     def trace_copy(k, slot):
         return pltpu.make_async_remote_copy(
@@ -317,7 +339,6 @@
         i = 2 * index(chip_rel(t // 2)) + t % 2
         rows = pl.ds(al(i * nb), nb)
         c_acc[:, rows] = -0.5 * (c_acc[:, rows] + nt(s_low[:, last], g[rows, last]))
-        finish(i).start()
 
     for k in range(1, 8):
         trace_copy(k, (pos + n_dev - k) % n_dev).wait_recv()
@@ -335,10 +356,6 @@
         passed(m, pass_from).wait_send()
         passed_shared(m, core).wait_send()
 
-    @pl.loop(0, order // nb)
-    def _(i):
-        finish(i).wait()
-
 
 def symmetric_shards(hamiltonian):
     nb, order = hamiltonian.shape
@@ -349,26 +366,25 @@
     sign_next, occupation = pl.pallas_call(
         kernel,
         out_shape=(
-            jax.ShapeDtypeStruct((nb, order), jnp.float32),
+            pltpu.VMEM((nb, order), jnp.float32),
             jax.ShapeDtypeStruct((8, 128), jnp.float32),
         ),
-        in_specs=[hbm, hbm],
-        out_specs=(hbm, pl.BlockSpec(memory_space=pltpu.VMEM)),
+        in_specs=[hbm],
+        out_specs=(pl.BlockSpec(memory_space=pltpu.VMEM), pl.BlockSpec(memory_space=pltpu.VMEM)),
         scratch_shapes=[
             pltpu.VMEM((order, order), jnp.bfloat16),
             pltpu.VMEM((nb, order), jnp.bfloat16),
             pltpu.VMEM((nb, order), jnp.float32),
-            pltpu.VMEM((nb, order), jnp.float32),
             pltpu.VMEM((cycle_size, 8, nb), jnp.float32),
-            dma((2,)), dma((cycle_size,)), dma, dma,
+            dma((4,)), dma, dma,
             six, six, six, six, three, three,
             six, six, six, six, three, three,
             seven, seven,
         ],
         compiler_params=pltpu.CompilerParams(
-            collective_id=0, has_side_effects=True, vmem_limit_bytes=67043328,
+            collective_id=0, has_side_effects=True, vmem_limit_bytes=50 * 2**20,
         ),
-    )(hamiltonian.astype(jnp.bfloat16), hamiltonian)
+    )(hamiltonian)
     return (sign_next, occupation[0, :1])
 
 

time: 98.9 us -> 80.4 us (0.81)
  Pallas kernels: 83 us -> 75 us
  other arithmetic: 6.03 us -> 0 us
  local copies, waits for them, and re-layouts: 8.97 us -> 4.58 us
    pallas_call x1, Pallas kernels: 83 us -> 75 us  [symmetric_shards(): pl.pallas_call(kernel, out_shape=(pltpu.VMEM((nb, order), jnp.float32), j...]
    convert_element_type x1 -> x0, other arithmetic: 6.03 us -> none  [symmetric_shards(): hamiltonian.astype(jnp.bfloat16)]
    unnamed x1, local copies, waits for them, and re-layouts: 7.77 us -> 3.4 us
where the time goes in v2:
time: 80.4 us; the launch traced here: 80.3 us
  Pallas kernels  75 us (93%)
  local copies, waits for them, and re-layouts  4.58 us (6%)
    pallas_call x1, Pallas kernels, symmetric_shards(): pl.pallas_call(kernel, out_shape=(pltpu.VMEM((nb, order), jnp.float32), j...  75 us
    unnamed x1, local copies, waits for them, and re-layouts  3.4 us

profile of v2, /device:TPU:0, one launch (start us, length us, event | category | flops | bytes accessed | tf_op | source)
XLA Modules:
  0.0 80.3 jit_solution(4299570688246487261)
XLA Ops:
  0.6 75.0 %shard_map.30 = (f32[512,4096]{1,0:T(8,128)S(1)}, f32[8,128]{1,0:T(8,128)}) custom-call(f32[512,4096]{1,0:T(8,128)} %ham_hbm.1), custom_call_target="tpu_custom_call" | custom-call | tf_op jit(solution)/shard_map/pallas_call | solution.py:366
  75.7 1.2 %slice.3 = f32[1,1]{1,0:T(1,128)} slice(f32[8,128]{1,0:T(8,128)} %get-tuple-element.5), slice={[0:1], [0:1]} | slice | bytes 8 | tf_op jit(solution)/shard_map/slice | solution.py:388
  76.9 3.4 %copy.4 = f32[512,4096]{1,0:T(8,128)} copy(f32[512,4096]{1,0:T(8,128)S(1)} %get-tuple-element.6) | data formatting | bytes 16777216

commit v3 on v2

--- a/solution.py
+++ b/solution.py
@@ -275,6 +275,11 @@
                 to = block(start + k)
                 c_acc[:, to] += nn(s_low[:, block(q)], g[block(q), to])
 
+    def trace_step(t, carry):
+        cols = block(2 * index(chip_rel(t // 2)) + t % 2)
+        product = s_low[:, cols].astype(f32) * left[:, cols].astype(f32)
+        return carry + jnp.sum(product, axis=0, keepdims=True)
+
     for b in range(2):
         forward_ready("x", 4 + b)
         forward_ready("y", 4 + b)
@@ -300,6 +305,7 @@
                 add_column(base + b, base)
         else:
             add_column(nx + b, nx)
+            tr_c = lax.fori_loop(0, 6, trace_step, jnp.zeros((1, nb), f32))
             for m in (1, 2, 3):
                 passed(m, far).wait_recv()
                 passed_shared(m, core).start()
@@ -312,12 +318,7 @@
     add_diagonal(s_acc, left, nf)
     s_low[:, last] = s_acc[:, last].astype(jnp.bfloat16)
 
-    def trace_step(t, carry):
-        cols = pl.ds(al(t * nb), nb)
-        product = s_low[:, cols].astype(f32) * left[:, cols].astype(f32)
-        return carry + jnp.sum(product, axis=0, keepdims=True)
-
-    tr_c = lax.fori_loop(0, order // nb, trace_step, jnp.zeros((1, nb), f32))
+    tr_c = lax.fori_loop(6, 8, trace_step, tr_c)
     tr[pos, 0:1, :] = 1.5 * tr[pos, 0:1, :] - 0.5 * tr_c
 
     for b in range(2):

time: 80.4 us -> 80.5 us (level)
  no operation moved by 1% of the time
where the time goes in v3:
time: 80.5 us; the launch traced here: 80.3 us
  Pallas kernels  75.1 us (93%)
  local copies, waits for them, and re-layouts  4.58 us (6%)
    pallas_call x1, Pallas kernels, symmetric_shards(): pl.pallas_call(kernel, out_shape=(pltpu.VMEM((nb, order), jnp.float32), j...  75.1 us
    unnamed x1, local copies, waits for them, and re-layouts  3.4 us

profile of v3, /device:TPU:0, one launch (start us, length us, event | category | flops | bytes accessed | tf_op | source)
XLA Modules:
  0.0 80.3 jit_solution(16238505992882951896)
XLA Ops:
  0.6 75.1 %shard_map.30 = (f32[512,4096]{1,0:T(8,128)S(1)}, f32[8,128]{1,0:T(8,128)}) custom-call(f32[512,4096]{1,0:T(8,128)} %ham_hbm.1), custom_call_target="tpu_custom_call" | custom-call | tf_op jit(solution)/shard_map/pallas_call | solution.py:367
  75.8 1.2 %slice.3 = f32[1,1]{1,0:T(1,128)} slice(f32[8,128]{1,0:T(8,128)} %get-tuple-element.5), slice={[0:1], [0:1]} | slice | bytes 8 | tf_op jit(solution)/shard_map/slice | solution.py:389
  77.0 3.4 %copy.4 = f32[512,4096]{1,0:T(8,128)} copy(f32[512,4096]{1,0:T(8,128)S(1)} %get-tuple-element.6) | data formatting | bytes 16777216
